TPU v7x, 32 devices: a whole 2x2x4 slice. The times are simulated.
32 devices in a mesh: dp: 8 (over y, x, core), mp: 4 (over z).
Axes of the slice: x: 2, y: 2, z: 4, core: 2. Of those that a mesh axis runs over, the one named last changes fastest.
Arguments:
- inputs: bfloat16 [1024, 6144], P('dp'), may hold values from -6 to 6
- pre_act: bfloat16 [1024, 12288], P('dp', 'mp'), may hold values from -6 to 6
- out_grad: bfloat16 [1024, 6144], P('dp'), may hold values from -6 to 6
- w_in: bfloat16 [6144, 12288], P(None, 'mp'), may hold values from -0.109375 to 0.109375
- w_out: bfloat16 [12288, 6144], P('mp'), may hold values from -0.0546875 to 0.0546875
- master_in: float32 [6144, 12288], P('dp', 'mp'), may hold values from -0.3 to 0.3
- master_out: float32 [12288, 6144], P('mp', 'dp'), may hold values from -0.3 to 0.3
- row_in: float32 [6144], P('dp'), may hold values from 12.8 to 686.08
- col_in: float32 [12288], P('mp'), may hold values from 25 to 128
- row_out: float32 [12288], P('mp'), may hold values from 25.6 to 1372.16
- col_out: float32 [6144], P('dp'), may hold values from 51 to 256
Outputs:
- input_grad: bfloat16 [1024, 6144], P('dp', 'mp')
- new_master_in: float32 [6144, 12288], P('dp', 'mp')
- new_master_out: float32 [12288, 6144], P('mp', 'dp')
All inputs are finite; a program needn't handle non-finite values.
Results may differ from a plain program's by a relative error of at most 0.012.
Values may be sent and summed in bfloat16 or wider, within the bound.
A program may use at most 256 MiB of HBM per device.

v0:
```python
import math
import jax
import jax.numpy as jnp
from jax import lax
from jax.experimental.layout import Layout, with_layout_constraint
from jax.sharding import PartitionSpec as P

D = 6144
FF = 12288
decay_rate = 0.8
step_size = 0.05
tiny_square = 1e-30


def gelu_parts(pre):
    cumulative = 0.5 * (1.0 + jax.scipy.special.erf(pre * (1.0 / math.sqrt(2.0))))
    density = jnp.exp(-0.5 * pre * pre) * (1.0 / math.sqrt(2.0 * math.pi))
    return (pre * cumulative, cumulative + pre * density)


def contract_rows(left, right):
    return lax.dot_general(
        left, right, (((0,), (0,)), ((), ())), preferred_element_type=jnp.float32
    )


def scatter_pieces(partial, axis):
    size = lax.axis_size(axis)
    me = lax.axis_index(axis)
    width = partial.shape[1] // size
    piece = lambda k: lax.dynamic_slice_in_dim(partial, k * width, width, 1)
    pieces = [piece(me)]
    for shift in range(1, size):
        moved = piece(lax.rem(me + shift, size)).astype(jnp.bfloat16)
        pieces.append(lax.ppermute(moved, axis, [(i, (i + shift) % size) for i in range(size)]))
    return pieces


def body(
    inputs, pre_act, out_grad, w_in, w_out, master_in, master_out, row_in, col_in, row_out, col_out
):
    active, slope = gelu_parts(pre_act.astype(jnp.float32))
    hidden = active.astype(jnp.bfloat16)
    hidden_all = lax.all_gather(hidden, "dp", axis=0, tiled=True)
    out_grad, _ = lax.optimization_barrier((out_grad, hidden))
    out_cols = lax.all_to_all(out_grad, "dp", 1, 0, tiled=True)
    hid_grad = lax.dot_general(
        out_grad, w_out, (((1,), (1,)), ((), ())), preferred_element_type=jnp.float32
    )
    pre_grad = (hid_grad * slope).astype(jnp.bfloat16)
    pre_grad_all = lax.all_gather(pre_grad, "dp", axis=0, tiled=True)
    input_part = lax.dot_general(
        pre_grad, w_in, (((1,), (1,)), ((), ())), preferred_element_type=jnp.float32
    )
    inputs, input_part = lax.optimization_barrier((inputs, input_part))
    in_cols = lax.all_to_all(inputs, "dp", 1, 0, tiled=True)
    pieces = scatter_pieces(input_part, "mp")
    grad_out = contract_rows(hidden_all, out_cols)
    square_out = grad_out * grad_out + tiny_square
    width_out, row_out_sum = lax.psum((jnp.sum(square_out, axis=0), jnp.sum(row_out)), "mp")
    cols_out = decay_rate * col_out + (1.0 - decay_rate) * width_out / FF
    hidden_out, sum_out = lax.psum((jnp.sum(square_out, axis=1), jnp.sum(width_out)), "dp")
    rows_out = decay_rate * row_out + (1.0 - decay_rate) * hidden_out / D
    mean_out = (decay_rate * row_out_sum + (1.0 - decay_rate) * sum_out / D) / FF
    update_out = grad_out / jnp.sqrt(rows_out[:, None] * cols_out[None, :] / mean_out)
    new_master_out = master_out - step_size * update_out
    pre_grad_all, new_master_out, pieces = lax.optimization_barrier(
        (pre_grad_all, new_master_out, pieces)
    )
    input_grad = sum((piece.astype(jnp.float32) for piece in pieces)).astype(jnp.bfloat16)
    grad_in = with_layout_constraint(contract_rows(in_cols, pre_grad_all), Layout((0, 1)))
    square_in = grad_in * grad_in + tiny_square
    width_in = lax.psum(jnp.sum(square_in, axis=1), "mp")
    rows_in = decay_rate * row_in + (1.0 - decay_rate) * width_in / FF
    hidden_in, sum_in = lax.psum((jnp.sum(square_in, axis=0), jnp.sum(rows_in)), "dp")
    cols_in = decay_rate * col_in + (1.0 - decay_rate) * hidden_in / D
    mean_in = sum_in / D
    update_in = grad_in / jnp.sqrt(rows_in[:, None] * cols_in[None, :] / mean_in)
    new_master_in = master_in - step_size * update_in
    return (input_grad, new_master_in, new_master_out)


def solution(mesh):
    in_specs = (
        P("dp", None),
        P("dp", "mp"),
        P("dp", None),
        P(None, "mp"),
        P("mp", None),
        P("dp", "mp"),
        P("mp", "dp"),
        P("dp"),
        P("mp"),
        P("mp"),
        P("dp"),
    )
    out_specs = (P("dp", "mp"), P("dp", "mp"), P("mp", "dp"))
    return jax.shard_map(body, mesh=mesh, in_specs=in_specs, out_specs=out_specs, check_vma=False)
```

profile of v0, /device:TPU:0, one launch (start us, length us, event | category | flops | bytes accessed | tf_op | source)
XLA Modules:
  0.0 233.9 jit_solution(13261236055143968567)
XLA Ops:
  7.2 0.0 all-gather.5.cloned.1.call-start
  7.2 2.4 %fusion.8 = bf16[128,3072]{1,0:T(8,128)(2,1)} fusion(bf16[128,3072]{1,0:T(8,128)(2,1)} %param.12), kind=kLoop, calls=%fused_computation.18 | loop fusion | flops 2359296 | bytes 1572864 | tf_op jit(solution)/shard_map/convert_element_type | solution.py:43
  9.6 0.0 all-gather.5.cloned.1.call-update
  9.6 0.0 copy-start.1
  9.6 0.0 all-gather.3.cloned.1.call-start
  9.7 22.5 %fusion.4 = bf16[128,3072]{1,0:T(8,128)(2,1)} fusion(bf16[128,6144]{1,0:T(8,128)(2,1)} %param.13, bf16[3072,6144]{1,0:T(8,128)(2,1)} %param.15, bf16[128,3072]{1,0:T(8,128)(2,1)} %param.12), kind=kOutput, calls=%fused_computation.9 | convolution fusion | flops 4836163584 | bytes 40894464 | tf_op jit(solution)/shard_map/dot_general | solution.py:47
  32.2 0.0 all-gather.3.cloned.1.call-update
  32.2 0.0 copy-done.1
  32.2 1.6 copy.14
  33.8 5.2 %all-to-all-start = ((bf16[128,8,768]{0,2,1:T(8,128)(2,1)}), bf16[128,8,768]{0,2,1:T(8,128)(2,1)}, u32[]{:S(2)}, u32[]{:S(2)}) async-start(bf16[128,8,768]{0,2,1:T(8,128)(2,1)} %bitcast), calls=%async_computation | async-start | bytes 3145728 | tf_op jit(solution)/shard_map/all_to_all | solution.py:46
  39.0 17.9 %fusion.13 = f32[128,6144]{1,0:T(8,128)S(1)} fusion(bf16[128,3072]{1,0:T(8,128)(2,1)} %fusion.4, bf16[6144,3072]{1,0:T(8,128)(2,1)} %param.14), kind=kOutput, calls=%fused_computation.32 | convolution fusion | flops 4831838208 | bytes 41680896 | tf_op jit(solution)/shard_map/dot_general | solution.py:52
  56.9 0.0 copy-start.2
  57.0 2.6 %copy.16 = bf16[128,6144]{0,1:T(8,128)(2,1)} copy(bf16[128,6144]{1,0:T(8,128)(2,1)} %param.11) | data formatting | bytes 3145728 | tf_op jit(solution)/shard_map/optimization_barrier | solution.py:55
  59.5 14.5 %all-to-all-done = bf16[128,8,768]{0,2,1:T(8,128)(2,1)} async-done(((bf16[128,8,768]{0,2,1:T(8,128)(2,1)}), bf16[128,8,768]{0,2,1:T(8,128)(2,1)}, u32[]{:S(2)}, u32[]{:S(2)}) %all-to-all-start) | async-done | bytes 1572896 | tf_op jit(solution)/shard_map/all_to_all | solution.py:46
  74.1 4.3 %all-to-all-start.1 = ((bf16[128,8,768]{0,2,1:T(8,128)(2,1)}), bf16[128,8,768]{0,2,1:T(8,128)(2,1)}, u32[]{:S(2)}, u32[]{:S(2)}) async-start(bf16[128,8,768]{0,2,1:T(8,128)(2,1)} %bitcast.14), calls=%async_computation.1 | async-start | bytes 3145728 | tf_op jit(solution)/shard_map/all_to_all | solution.py:56
  78.4 1.1 dynamic-slice_convert_fusion
  79.4 3.3 %collective-permute-start.2 = (bf16[128,1536]{1,0:T(8,128)(2,1)}, bf16[128,1536]{1,0:T(8,128)(2,1)S(1)}, u32[]{:S(2)}, u32[]{:S(2)}) collective-permute-start(bf16[128,1536]{1,0:T(8,128)(2,1)} %get-tuple-element.33), channel_id=1, source_target_pairs={{0,3},{1,0},{2,1},{3,2},{4,7},{5,4},{6,5},{7,6},{8,11},{9,8},{10,9... | collective-permute-start | bytes 1179656 | tf_op jit(solution)/shard_map/ppermute | solution.py:35
  82.8 0.0 collective-permute-start.1
  82.8 1.1 collective-permute-start
  83.9 0.0 copy-done.2
  83.9 0.6 reduce_sum.65
  84.5 1.0 constant_dynamic-slice_fusion
  85.4 2.6 %copy.15 = bf16[8,128,768]{2,1,0:T(8,128)(2,1)} copy(bf16[8,128,768]{1,2,0:T(8,128)(2,1)} %bitcast.1) | data formatting | bytes 3145728 | tf_op jit(solution)/shard_map/all_to_all | solution.py:46
  88.0 19.7 %all-to-all-done.1 = bf16[128,8,768]{0,2,1:T(8,128)(2,1)} async-done(((bf16[128,8,768]{0,2,1:T(8,128)(2,1)}), bf16[128,8,768]{0,2,1:T(8,128)(2,1)}, u32[]{:S(2)}, u32[]{:S(2)}) %all-to-all-start.1) | async-done | bytes 1572896 | tf_op jit(solution)/shard_map/all_to_all | solution.py:56
  107.7 1.7 copy.17
  109.5 0.0 all-gather.5.cloned.1.call-done
  109.5 0.0 copy-start.4
  109.5 10.4 %fusion.1 = (f32[3072]{0:T(1024)S(1)}, f32[768]{0:T(1024)S(1)}, f32[3072,768]{1,0:T(8,128)}) fusion(bf16[1024,3072]{1,0:T(8,128)(2,1)} %all-gather.5.cloned.1.call-done, bf16[1024,768]{1,0:T(8,128)(2,1)} %bitcast.16), kind=kOutput, calls=%fused_computation.5 | convolution fusion | flops 4841271296 | bytes 17316864 | tf_op jit(solution)/shard_map/dot_general | solution.py:22
  119.9 12.4 %all-reduce.2 = (f32[]{:T(128)}, f32[768]{0:T(1024)S(1)}) all-reduce(f32[]{:T(128)} %reduce_sum.65, f32[768]{0:T(1024)S(1)} %get-tuple-element.24), channel_id=1, replica_groups=mesh['dp'=8,'mp'=4] {'mp'}, use_global_device_ids=true, to_apply=%region_5.0 | all-reduce | flops 769 | bytes 6152 | tf_op jit(solution)/shard_map/psum | solution.py:60
  132.4 0.0 copy-done.4
  132.4 0.6 multiply_add_fusion.5
  133.0 23.4 %all-reduce.1 = (f32[]{:T(128)}, f32[3072]{0:T(1024)S(1)}) all-reduce(f32[]{:T(128)} %get-tuple-element.37, f32[3072]{0:T(1024)S(1)} %get-tuple-element.23), channel_id=1, replica_groups=mesh['dp'=8,'mp'=4] {'dp'}, use_global_device_ids=true, to_apply=%region_7.0 | all-reduce | flops 3073 | bytes 24584 | tf_op jit(solution)/shard_map/psum | solution.py:62
  157.7 11.2 %multiply_subtract_fusion.1 = f32[3072,768]{1,0:T(8,128)} fusion(f32[3072,768]{1,0:T(8,128)} %param.17, f32[3072,768]{1,0:T(8,128)} %get-tuple-element.38, f32[]{:T(128)S(6)} %div.48, f32[768]{0:T(1024)S(1)} %get-tuple-element.36, f32[3072]{0:T(1024)S(1)} %multiply_add_fusion.3), kind=kLoop, calls=%fused_computation.2 | loop fusion | flops 11796480 | bytes 28326916 | tf_op jit(solution)/shard_map/sub | solution.py:66
  169.0 0.0 collective-permute-done.2
  169.0 0.0 collective-permute-done.1
  169.0 0.0 collective-permute-done
  169.0 0.0 all-gather.3.cloned.1.call-done
  169.0 0.0 copy-start.5
  169.0 0.0 copy-start.3
  169.0 0.0 copy-start
  169.0 11.3 %fusion.2 = (f32[3072]{0:T(1024)S(1)}, f32[768]{0:T(1024)S(1)}, f32[768,3072]{1,0:T(8,128)}) fusion(bf16[1024,768]{1,0:T(8,128)(2,1)S(1)} %bitcast.15, bf16[1024,3072]{1,0:T(8,128)(2,1)} %all-gather.3.cloned.1.call-done), kind=kOutput, calls=%fused_computation.6 | convolution fusion | flops 4841271296 | bytes 17316864 | tf_op jit(solution)/shard_map/dot_general | solution.py:22
  180.3 8.3 %psum.53 = f32[768]{0:T(1024)S(1)} all-reduce(f32[768]{0:T(1024)S(1)} %get-tuple-element.22), channel_id=1, replica_groups=mesh['dp'=8,'mp'=4] {'mp'}, use_global_device_ids=true, to_apply=%region_9.0 | all-reduce | flops 768 | bytes 6144 | tf_op jit(solution)/shard_map/psum | solution.py:73
  188.6 0.0 copy-done.5
  188.6 0.6 fusion.12
  189.2 23.4 %all-reduce = (f32[]{:T(128)}, f32[3072]{0:T(1024)S(1)}) all-reduce(f32[]{:T(128)} %get-tuple-element.31, f32[3072]{0:T(1024)S(1)} %get-tuple-element.21), channel_id=1, replica_groups=mesh['dp'=8,'mp'=4] {'dp'}, use_global_device_ids=true, to_apply=%region_13.0 | all-reduce | flops 3073 | bytes 24584 | tf_op jit(solution)/shard_map/psum | solution.py:75
  213.3 0.0 copy-done.3
  213.3 0.0 copy-done
  213.3 2.0 add_convert_fusion
  215.3 11.7 %multiply_subtract_fusion = f32[768,3072]{1,0:T(8,128)} fusion(f32[768,3072]{1,0:T(8,128)} %param.16, f32[768,3072]{1,0:T(8,128)} %get-tuple-element.39, f32[]{:T(128)S(6)} %div.54, f32[3072]{0:T(1024)S(1)} %multiply_add_fusion.2, f32[768]{0:T(1024)S(1)} %get-tuple-element.32), kind=kLoop, calls=%fused_computation | loop fusion | flops 11796480 | bytes 28326916 | tf_op jit(solution)/shard_map/sub | solution.py:79
  (2 shorter events, 0.0 us)
Async XLA Ops:
  7.2 102.3 %all-gather.5.cloned.1.call-start = ((), (), s32[]{:S(2)}) async-start(), calls=%async_computation.3 | async-start | bytes 7077888 | tf_op jit(solution)/shard_map/all_gather | solution.py:44
  9.6 22.6 %copy-start.1 = (bf16[128,6144]{1,0:T(8,128)(2,1)S(1)}, bf16[128,6144]{1,0:T(8,128)(2,1)}, u32[]{:S(2)}) copy-start(bf16[128,6144]{1,0:T(8,128)(2,1)} %param.13) | copy-start | bytes 4718596
  9.6 159.4 %all-gather.3.cloned.1.call-start = ((), (), s32[]{:S(2)}) async-start(), calls=%async_computation.2 | async-start | bytes 7077888 | tf_op jit(solution)/shard_map/all_gather | solution.py:51
  33.8 40.2 %all-to-all-start = ((bf16[128,8,768]{0,2,1:T(8,128)(2,1)}), bf16[128,8,768]{0,2,1:T(8,128)(2,1)}, u32[]{:S(2)}, u32[]{:S(2)}) async-start(bf16[128,8,768]{0,2,1:T(8,128)(2,1)} %bitcast), calls=%async_computation | async-start | bytes 3145728 | tf_op jit(solution)/shard_map/all_to_all | solution.py:46
  56.9 26.9 %copy-start.2 = (f32[3072]{0:T(1024)S(1)}, f32[3072]{0:T(1024)}, u32[]{:S(2)}) copy-start(f32[3072]{0:T(1024)} %param.20) | copy-start | bytes 36868
  74.1 33.7 %all-to-all-start.1 = ((bf16[128,8,768]{0,2,1:T(8,128)(2,1)}), bf16[128,8,768]{0,2,1:T(8,128)(2,1)}, u32[]{:S(2)}, u32[]{:S(2)}) async-start(bf16[128,8,768]{0,2,1:T(8,128)(2,1)} %bitcast.14), calls=%async_computation.1 | async-start | bytes 3145728 | tf_op jit(solution)/shard_map/all_to_all | solution.py:56
  79.4 89.5 %collective-permute-start.2 = (bf16[128,1536]{1,0:T(8,128)(2,1)}, bf16[128,1536]{1,0:T(8,128)(2,1)S(1)}, u32[]{:S(2)}, u32[]{:S(2)}) collective-permute-start(bf16[128,1536]{1,0:T(8,128)(2,1)} %get-tuple-element.33), channel_id=1, source_target_pairs={{0,3},{1,0},{2,1},{3,2},{4,7},{5,4},{6,5},{7,6},{8,11},{9,8},{10,9... | collective-permute-start | bytes 1179656 | tf_op jit(solution)/shard_map/ppermute | solution.py:35
  82.8 86.2 %collective-permute-start.1 = (bf16[128,1536]{1,0:T(8,128)(2,1)}, bf16[128,1536]{1,0:T(8,128)(2,1)}, u32[]{:S(2)}, u32[]{:S(2)}) collective-permute-start(bf16[128,1536]{1,0:T(8,128)(2,1)} %get-tuple-element.34), channel_id=1, source_target_pairs={{0,2},{1,3},{2,0},{3,1},{4,6},{5,7},{6,4},{7,5},{8,10},{9,11},{10,... | collective-permute-start | bytes 1179656 | tf_op jit(solution)/shard_map/ppermute | solution.py:35
  82.8 86.2 %collective-permute-start = (bf16[128,1536]{1,0:T(8,128)(2,1)}, bf16[128,1536]{1,0:T(8,128)(2,1)}, u32[]{:S(2)}, u32[]{:S(2)}) collective-permute-start(bf16[128,1536]{1,0:T(8,128)(2,1)} %get-tuple-element.35), channel_id=1, source_target_pairs={{0,1},{1,2},{2,3},{3,0},{4,5},{5,6},{6,7},{7,4},{8,9},{9,10},{10,1... | collective-permute-start | bytes 1179656 | tf_op jit(solution)/shard_map/ppermute | solution.py:35
  109.5 22.9 %copy-start.4 = (f32[768]{0:T(1024)S(1)}, f32[768]{0:T(1024)}, u32[]{:S(2)}) copy-start(f32[768]{0:T(1024)} %param.21) | copy-start | bytes 9220
  169.0 19.6 %copy-start.5 = (f32[768]{0:T(1024)S(1)}, f32[768]{0:T(1024)}, u32[]{:S(2)}) copy-start(f32[768]{0:T(1024)} %param.18) | copy-start | bytes 9220
  169.0 44.2 %copy-start.3 = (f32[3072]{0:T(1024)S(1)}, f32[3072]{0:T(1024)}, u32[]{:S(2)}) copy-start(f32[3072]{0:T(1024)} %param.19) | copy-start | bytes 36868
  169.0 44.2 %copy-start = (f32[128,1536]{1,0:T(8,128)S(1)}, f32[128,1536]{1,0:T(8,128)}, u32[]{:S(2)}) copy-start(f32[128,1536]{1,0:T(8,128)} %constant_dynamic-slice_fusion) | copy-start | bytes 2359300
Sparse Core Ops, SparseCore 0:
  9.9 61.8 all-gather.4
  73.7 59.2 all-gather.2
where the time goes:
time: 234 us
  blocking collectives  67.5 us (29%)
  matrix products  62.1 us (27%)
  waiting for transfers between devices  34.3 us (15%)
  other arithmetic  29.2 us (12%)
  between operations  16.2 us (7%)
  starting transfers between devices  14 us (6%)
  local copies, waits for them, and re-layouts  10.5 us (4%)
    psum x1, blocking collectives, body(): lax.psum((jnp.sum(square_out, axis=1), jnp.sum(width_out)), 'dp')  23.4 us
    psum x1, blocking collectives, body(): lax.psum((jnp.sum(square_in, axis=0), jnp.sum(rows_in)), 'dp')  23.4 us
    dot_general x1, matrix products, body(): lax.dot_general(out_grad, w_out, (((1,), (1,)), ((), ())), preferred_elem...  22.5 us
    dot_general x2, matrix products, contract_rows(): lax.dot_general(left, right, (((0,), (0,)), ((), ())), preferred_element_...  21.7 us
    all_to_all x1, waiting for transfers between devices, body(): in_cols = lax.all_to_all(inputs, 'dp', 1, 0, tiled=True)  19.7 us
    dot_general x1, matrix products, body(): lax.dot_general(pre_grad, w_in, (((1,), (1,)), ((), ())), preferred_eleme...  17.9 us
    all_to_all x1, waiting for transfers between devices, body(): out_cols = lax.all_to_all(out_grad, 'dp', 1, 0, tiled=True)  14.5 us
    psum x1, blocking collectives, body(): lax.psum((jnp.sum(square_out, axis=0), jnp.sum(row_out)), 'mp')  12.4 us
  transfers between devices with their start and end apart: 7, of which 2 were waited for; matrix products, arithmetic and copies ran while one was open for 32% of the time, Pallas kernels for 0%

commit v1 on v0

--- a/solution.py
+++ b/solution.py
@@ -53,7 +53,10 @@
         pre_grad, w_in, (((1,), (1,)), ((), ())), preferred_element_type=jnp.float32
     )
     inputs, input_part = lax.optimization_barrier((inputs, input_part))
-    in_cols = lax.all_to_all(inputs, "dp", 1, 0, tiled=True)
+    peers = lax.axis_size("dp")
+    blocks = jnp.stack(jnp.split(inputs, peers, axis=1), axis=0)
+    blocks = lax.all_to_all(blocks, "dp", split_axis=0, concat_axis=0)
+    in_cols = jnp.concatenate(blocks, axis=0)
     pieces = scatter_pieces(input_part, "mp")
     grad_out = contract_rows(hidden_all, out_cols)
     square_out = grad_out * grad_out + tiny_square

time: 234 us -> 208 us (0.89)
  waiting for transfers between devices: 34.3 us -> 0.07 us
  local copies, waits for them, and re-layouts: 10.5 us -> 19.2 us
    all_to_all x1, waiting for transfers between devices: 19.7 us -> 0.01 us  [body(): blocks = lax.all_to_all(blocks, 'dp', split_axis=0, concat_axis=0)]
    all_to_all x1, waiting for transfers between devices: 14.5 us -> 0.01 us  [body(): out_cols = lax.all_to_all(out_grad, 'dp', 1, 0, tiled=True)]
    unnamed x12 -> x21, local copies, waits for them, and re-layouts: 0.04 us -> 11.4 us
    dot_general x1, matrix products: 22.5 us -> 19.9 us  [body(): lax.dot_general(out_grad, w_out, (((1,), (1,)), ((), ())), preferred_elem...]
    optimization_barrier x1 -> x0, local copies, waits for them, and re-layouts: 2.58 us -> none  [body(): inputs, input_part = lax.optimization_barrier((inputs, input_part))]
  transfers between devices with their start and end apart: 7 -> 7, of which waited for: 2 -> 0; matrix products, arithmetic and copies ran while one was open for 32% -> 39% of each run, Pallas kernels for 0% -> 0%
where the time goes in v1:
time: 208 us
  blocking collectives  68.1 us (33%)
  matrix products  61 us (29%)
  other arithmetic  29.5 us (14%)
  local copies, waits for them, and re-layouts  19.2 us (9%)
  between operations  16 us (8%)
  starting transfers between devices  13.8 us (7%)
    psum x1, blocking collectives, body(): lax.psum((jnp.sum(square_out, axis=1), jnp.sum(width_out)), 'dp')  25 us
    psum x1, blocking collectives, body(): lax.psum((jnp.sum(square_in, axis=0), jnp.sum(rows_in)), 'dp')  23.4 us
    dot_general x2, matrix products, contract_rows(): lax.dot_general(left, right, (((0,), (0,)), ((), ())), preferred_element_...  22.1 us
    dot_general x1, matrix products, body(): lax.dot_general(out_grad, w_out, (((1,), (1,)), ((), ())), preferred_elem...  19.9 us
    dot_general x1, matrix products, body(): lax.dot_general(pre_grad, w_in, (((1,), (1,)), ((), ())), preferred_eleme...  19 us
    sub x1, other arithmetic, body(): new_master_in = master_in - step_size * update_in  11.7 us
    unnamed x21, local copies, waits for them, and re-layouts  11.4 us
    psum x1, blocking collectives, body(): lax.psum((jnp.sum(square_out, axis=0), jnp.sum(row_out)), 'mp')  11.4 us
  transfers between devices with their start and end apart: 7, of which 0 were waited for; matrix products, arithmetic and copies ran while one was open for 39% of the time, Pallas kernels for 0%

profile of v1, /device:TPU:0, one launch (start us, length us, event | category | flops | bytes accessed | tf_op | source)
XLA Modules:
  0.0 207.8 jit_solution(2293769981630615319)
XLA Ops:
  7.2 0.0 copy-start.2
  7.2 0.0 copy-start.1
  7.2 0.0 all-gather.5.cloned.1.call-start
  7.2 2.5 %fusion.8 = bf16[128,3072]{1,0:T(8,128)(2,1)} fusion(bf16[128,3072]{1,0:T(8,128)(2,1)} %param.12), kind=kLoop, calls=%fused_computation.18 | loop fusion | flops 2359296 | bytes 1572864 | tf_op jit(solution)/shard_map/convert_element_type | solution.py:43
  9.7 0.0 all-gather.5.cloned.1.call-update
  9.8 0.0 all-gather.3.cloned.1.call-start
  9.8 0.0 copy-done.2
  9.8 0.0 copy-done.1
  9.8 19.9 %fusion.4 = bf16[128,3072]{1,0:T(8,128)(2,1)} fusion(bf16[128,6144]{1,0:T(8,128)(2,1)S(1)} %copy-done.1, bf16[3072,6144]{1,0:T(8,128)(2,1)} %param.15, bf16[128,3072]{1,0:T(8,128)(2,1)S(1)} %copy-done.2), kind=kOutput, calls=%fused_computation.9 | convolution fusion | flops 4836163584 | bytes 40894464 | tf_op jit(solution)/shard_map/dot_general | solution.py:47
  29.8 0.0 all-gather.3.cloned.1.call-update
  29.8 1.6 copy.14
  31.4 4.9 %all-to-all-start = ((bf16[128,8,768]{0,2,1:T(8,128)(2,1)}), bf16[128,8,768]{0,2,1:T(8,128)(2,1)}, u32[]{:S(2)}, u32[]{:S(2)}) async-start(bf16[128,8,768]{0,2,1:T(8,128)(2,1)} %bitcast), calls=%async_computation | async-start | bytes 3145728 | tf_op jit(solution)/shard_map/all_to_all | solution.py:46
  36.3 19.0 %fusion.13 = f32[128,6144]{1,0:T(8,128)S(1)} fusion(bf16[128,3072]{1,0:T(8,128)(2,1)} %fusion.4, bf16[6144,3072]{1,0:T(8,128)(2,1)} %param.14), kind=kOutput, calls=%fused_computation.40 | convolution fusion | flops 4831838208 | bytes 41680896 | tf_op jit(solution)/shard_map/dot_general | solution.py:52
  55.2 0.0 copy-start.3
  55.3 1.1 dynamic-slice_convert_fusion
  56.3 4.0 %collective-permute-start.2 = (bf16[128,1536]{1,0:T(8,128)(2,1)}, bf16[128,1536]{1,0:T(8,128)(2,1)S(1)}, u32[]{:S(2)}, u32[]{:S(2)}) collective-permute-start(bf16[128,1536]{1,0:T(8,128)(2,1)} %get-tuple-element.33), channel_id=1, source_target_pairs={{0,3},{1,0},{2,1},{3,2},{4,7},{5,4},{6,5},{7,6},{8,11},{9,8},{10,9... | collective-permute-start | bytes 1179656 | tf_op jit(solution)/shard_map/ppermute | solution.py:35
  60.3 0.0 collective-permute-start.1
  60.3 1.1 collective-permute-start
  61.4 0.0 copy-done.3
  61.4 0.6 reduce_sum.65
  62.0 1.6 bitcast_dynamic-update-slice_fusion.7
  63.6 1.6 bitcast_dynamic-update-slice_fusion.6
  65.2 1.7 bitcast_dynamic-update-slice_fusion.5
  66.9 1.6 bitcast_dynamic-update-slice_fusion.4
  68.5 1.6 bitcast_dynamic-update-slice_fusion.3
  70.2 1.6 bitcast_dynamic-update-slice_fusion.2
  71.8 1.6 bitcast_dynamic-update-slice_fusion.1
  73.4 1.6 bitcast_dynamic-update-slice_fusion
  75.0 1.0 constant_dynamic-slice_fusion
  76.0 0.0 all-to-all-done
  76.0 3.8 %all-to-all-start.1 = ((bf16[8,128,768]{2,1,0:T(8,128)(2,1)}), bf16[8,128,768]{2,1,0:T(8,128)(2,1)S(1)}, u32[]{:S(2)}, u32[]{:S(2)}) async-start(bf16[8,128,768]{2,1,0:T(8,128)(2,1)} %bitcast_dynamic-update-slice_fusion), calls=%async_computation.1 | async-start | bytes 3145728 | tf_op jit(solution)/shard_map/all_to_all | solution.py:58
  79.8 2.6 %copy.15 = bf16[8,128,768]{2,1,0:T(8,128)(2,1)} copy(bf16[8,128,768]{1,2,0:T(8,128)(2,1)} %bitcast.1) | data formatting | bytes 3145728 | tf_op jit(solution)/shard_map/all_to_all | solution.py:46
  82.4 0.0 all-gather.5.cloned.1.call-done
  82.4 0.0 copy-start.5
  82.4 10.9 %fusion.1 = (f32[3072]{0:T(1024)S(1)}, f32[768]{0:T(1024)S(1)}, f32[3072,768]{1,0:T(8,128)}) fusion(bf16[1024,3072]{1,0:T(8,128)(2,1)} %all-gather.5.cloned.1.call-done, bf16[1024,768]{1,0:T(8,128)(2,1)} %bitcast.29), kind=kOutput, calls=%fused_computation.5 | convolution fusion | flops 4841271296 | bytes 17316864 | tf_op jit(solution)/shard_map/dot_general | solution.py:22
  93.2 11.4 %all-reduce.2 = (f32[]{:T(128)}, f32[768]{0:T(1024)S(1)}) all-reduce(f32[]{:T(128)} %reduce_sum.65, f32[768]{0:T(1024)S(1)} %get-tuple-element.24), channel_id=1, replica_groups=mesh['dp'=8,'mp'=4] {'mp'}, use_global_device_ids=true, to_apply=%region_5.0 | all-reduce | flops 769 | bytes 6152 | tf_op jit(solution)/shard_map/psum | solution.py:63
  104.6 0.0 copy-done.5
  104.6 0.7 multiply_add_fusion.5
  105.3 25.0 %all-reduce.1 = (f32[]{:T(128)}, f32[3072]{0:T(1024)S(1)}) all-reduce(f32[]{:T(128)} %get-tuple-element.37, f32[3072]{0:T(1024)S(1)} %get-tuple-element.23), channel_id=1, replica_groups=mesh['dp'=8,'mp'=4] {'dp'}, use_global_device_ids=true, to_apply=%region_7.0 | all-reduce | flops 3073 | bytes 24584 | tf_op jit(solution)/shard_map/psum | solution.py:65
  131.5 11.3 %multiply_subtract_fusion.1 = f32[3072,768]{1,0:T(8,128)} fusion(f32[3072,768]{1,0:T(8,128)} %param.17, f32[3072,768]{1,0:T(8,128)} %get-tuple-element.38, f32[]{:T(128)S(6)} %div.48, f32[768]{0:T(1024)S(1)} %get-tuple-element.36, f32[3072]{0:T(1024)S(1)} %multiply_add_fusion.3), kind=kLoop, calls=%fused_computation.2 | loop fusion | flops 11796480 | bytes 28326916 | tf_op jit(solution)/shard_map/sub | solution.py:69
  142.8 0.0 collective-permute-done.2
  142.8 0.0 collective-permute-done.1
  142.8 0.0 collective-permute-done
  142.8 0.0 all-gather.3.cloned.1.call-done
  142.9 0.0 all-to-all-done.1
  142.9 0.0 copy-start.6
  142.9 0.0 copy-start.4
  142.9 0.0 copy-start
  142.9 11.3 %fusion.2 = (f32[3072]{0:T(1024)S(1)}, f32[768]{0:T(1024)S(1)}, f32[768,3072]{1,0:T(8,128)}) fusion(bf16[1024,768]{1,0:T(8,128)(2,1)S(1)} %bitcast.28, bf16[1024,3072]{1,0:T(8,128)(2,1)} %all-gather.3.cloned.1.call-done), kind=kOutput, calls=%fused_computation.6 | convolution fusion | flops 4841271296 | bytes 17316864 | tf_op jit(solution)/shard_map/dot_general | solution.py:22
  154.2 8.3 %psum.53 = f32[768]{0:T(1024)S(1)} all-reduce(f32[768]{0:T(1024)S(1)} %get-tuple-element.22), channel_id=1, replica_groups=mesh['dp'=8,'mp'=4] {'mp'}, use_global_device_ids=true, to_apply=%region_9.0 | all-reduce | flops 768 | bytes 6144 | tf_op jit(solution)/shard_map/psum | solution.py:76
  162.5 0.0 copy-done.6
  162.5 0.6 fusion.12
  163.1 23.4 %all-reduce = (f32[]{:T(128)}, f32[3072]{0:T(1024)S(1)}) all-reduce(f32[]{:T(128)} %get-tuple-element.31, f32[3072]{0:T(1024)S(1)} %get-tuple-element.21), channel_id=1, replica_groups=mesh['dp'=8,'mp'=4] {'dp'}, use_global_device_ids=true, to_apply=%region_13.0 | all-reduce | flops 3073 | bytes 24584 | tf_op jit(solution)/shard_map/psum | solution.py:78
  187.1 0.0 copy-done.4
  187.2 0.0 copy-done
  187.2 2.0 add_convert_fusion
  189.2 11.7 %multiply_subtract_fusion = f32[768,3072]{1,0:T(8,128)} fusion(f32[768,3072]{1,0:T(8,128)} %param.16, f32[768,3072]{1,0:T(8,128)} %get-tuple-element.39, f32[]{:T(128)S(6)} %div.54, f32[3072]{0:T(1024)S(1)} %multiply_add_fusion.2, f32[768]{0:T(1024)S(1)} %get-tuple-element.32), kind=kLoop, calls=%fused_computation | loop fusion | flops 11796480 | bytes 28326916 | tf_op jit(solution)/shard_map/sub | solution.py:82
  (2 shorter events, 0.0 us)
Async XLA Ops:
  7.2 2.7 %copy-start.2 = (bf16[128,3072]{1,0:T(8,128)(2,1)S(1)}, bf16[128,3072]{1,0:T(8,128)(2,1)}, u32[]{:S(2)}) copy-start(bf16[128,3072]{1,0:T(8,128)(2,1)} %param.12) | copy-start | bytes 2359300
  7.2 2.7 %copy-start.1 = (bf16[128,6144]{1,0:T(8,128)(2,1)S(1)}, bf16[128,6144]{1,0:T(8,128)(2,1)}, u32[]{:S(2)}) copy-start(bf16[128,6144]{1,0:T(8,128)(2,1)} %param.13) | copy-start | bytes 4718596
  7.2 75.2 %all-gather.5.cloned.1.call-start = ((), (), s32[]{:S(2)}) async-start(), calls=%async_computation.3 | async-start | bytes 7077888 | tf_op jit(solution)/shard_map/all_gather | solution.py:44
  9.8 133.1 %all-gather.3.cloned.1.call-start = ((), (), s32[]{:S(2)}) async-start(), calls=%async_computation.2 | async-start | bytes 7077888 | tf_op jit(solution)/shard_map/all_gather | solution.py:51
  31.4 44.6 %all-to-all-start = ((bf16[128,8,768]{0,2,1:T(8,128)(2,1)}), bf16[128,8,768]{0,2,1:T(8,128)(2,1)}, u32[]{:S(2)}, u32[]{:S(2)}) async-start(bf16[128,8,768]{0,2,1:T(8,128)(2,1)} %bitcast), calls=%async_computation | async-start | bytes 3145728 | tf_op jit(solution)/shard_map/all_to_all | solution.py:46
  55.2 6.2 %copy-start.3 = (f32[3072]{0:T(1024)S(1)}, f32[3072]{0:T(1024)}, u32[]{:S(2)}) copy-start(f32[3072]{0:T(1024)} %param.20) | copy-start | bytes 36868
  56.3 86.5 %collective-permute-start.2 = (bf16[128,1536]{1,0:T(8,128)(2,1)}, bf16[128,1536]{1,0:T(8,128)(2,1)S(1)}, u32[]{:S(2)}, u32[]{:S(2)}) collective-permute-start(bf16[128,1536]{1,0:T(8,128)(2,1)} %get-tuple-element.33), channel_id=1, source_target_pairs={{0,3},{1,0},{2,1},{3,2},{4,7},{5,4},{6,5},{7,6},{8,11},{9,8},{10,9... | collective-permute-start | bytes 1179656 | tf_op jit(solution)/shard_map/ppermute | solution.py:35
  60.3 82.5 %collective-permute-start.1 = (bf16[128,1536]{1,0:T(8,128)(2,1)}, bf16[128,1536]{1,0:T(8,128)(2,1)}, u32[]{:S(2)}, u32[]{:S(2)}) collective-permute-start(bf16[128,1536]{1,0:T(8,128)(2,1)} %get-tuple-element.34), channel_id=1, source_target_pairs={{0,2},{1,3},{2,0},{3,1},{4,6},{5,7},{6,4},{7,5},{8,10},{9,11},{10,... | collective-permute-start | bytes 1179656 | tf_op jit(solution)/shard_map/ppermute | solution.py:35
  60.3 82.5 %collective-permute-start = (bf16[128,1536]{1,0:T(8,128)(2,1)}, bf16[128,1536]{1,0:T(8,128)(2,1)}, u32[]{:S(2)}, u32[]{:S(2)}) collective-permute-start(bf16[128,1536]{1,0:T(8,128)(2,1)} %get-tuple-element.35), channel_id=1, source_target_pairs={{0,1},{1,2},{2,3},{3,0},{4,5},{5,6},{6,7},{7,4},{8,9},{9,10},{10,1... | collective-permute-start | bytes 1179656 | tf_op jit(solution)/shard_map/ppermute | solution.py:35
  76.0 66.9 %all-to-all-start.1 = ((bf16[8,128,768]{2,1,0:T(8,128)(2,1)}), bf16[8,128,768]{2,1,0:T(8,128)(2,1)S(1)}, u32[]{:S(2)}, u32[]{:S(2)}) async-start(bf16[8,128,768]{2,1,0:T(8,128)(2,1)} %bitcast_dynamic-update-slice_fusion), calls=%async_computation.1 | async-start | bytes 3145728 | tf_op jit(solution)/shard_map/all_to_all | solution.py:58
  82.4 22.3 %copy-start.5 = (f32[768]{0:T(1024)S(1)}, f32[768]{0:T(1024)}, u32[]{:S(2)}) copy-start(f32[768]{0:T(1024)} %param.21) | copy-start | bytes 9220
  142.9 19.6 %copy-start.6 = (f32[768]{0:T(1024)S(1)}, f32[768]{0:T(1024)}, u32[]{:S(2)}) copy-start(f32[768]{0:T(1024)} %param.18) | copy-start | bytes 9220
  142.9 44.2 %copy-start.4 = (f32[3072]{0:T(1024)S(1)}, f32[3072]{0:T(1024)}, u32[]{:S(2)}) copy-start(f32[3072]{0:T(1024)} %param.19) | copy-start | bytes 36868
  142.9 44.3 %copy-start = (f32[128,1536]{1,0:T(8,128)S(1)}, f32[128,1536]{1,0:T(8,128)}, u32[]{:S(2)}) copy-start(f32[128,1536]{1,0:T(8,128)} %constant_dynamic-slice_fusion) | copy-start | bytes 2359300
Sparse Core Ops, SparseCore 0:
  9.9 64.6 all-gather.4
  76.5 57.3 all-gather.2
